TPU v7x, 32 devices: a whole 2x2x4 slice. The times are simulated.
32 devices in a mesh: seq: 4 (over y, x), blk: 8 (over z, core).
Axes of the slice: x: 2, y: 2, z: 4, core: 2. Of those that a mesh axis runs over, the one named last changes fastest.
Arguments:
- queries: bfloat16 [4, 2048, 2048], P('seq', 'blk'), may hold values from -150 to 150
- keys: bfloat16 [4, 256, 2048], P('seq', 'blk'), may hold values from -6 to 6
- values: bfloat16 [4, 256, 2048], P('seq', 'blk'), may hold values from -6 to 6
- image_index: int32 [4, 2048], P('seq', 'blk'), may hold values from 0 to 3, as said below
- head_gate: float32 [16], replicated, may hold values from 0.3 to 1.5
- out_weight: bfloat16 [2048, 4096], P(None, 'blk'), may hold values from -0.125 to 0.125
Outputs:
- layer_out: bfloat16 [4, 2048, 4096], P('seq', 'blk')
Inputs may be any that keep to these rules, and one draw needn't show every extreme that they name: Along each sequence image_index never falls; each image's run of text tokens is at least 256 long, so one device's tokens meet at most two images.
All inputs are finite; a program needn't handle non-finite values.
Results may differ from a plain program's by a relative error of at most 0.008.
Values may be sent and summed in bfloat16 or wider, within the bound.
No kernel may reach another device: no remote copies, remote signals or barrier semaphores. Data moves between devices by JAX's collectives and lax.ppermute only.
A program may use at most 128 MiB of HBM per device.

v0:
```python
import jax
import jax.numpy as jnp
from jax import lax
from jax.sharding import PartitionSpec as P

IMAGES = 4


def update(state_in, query_heads, images, key_rows, value_rows, image_rows):
    running_max, running_sum, weighted = state_in
    count = key_rows.shape[0]
    heads = query_heads.shape[1]
    head_size = query_heads.shape[2]
    key_heads = key_rows.reshape(count, heads, head_size)
    value_heads = value_rows.reshape(count, heads, head_size)
    scores = jnp.einsum(
        "thd,lhd->thl", query_heads, key_heads, preferred_element_type=jnp.float32
    ) * head_size ** (-0.5)
    latent_image = lax.iota(jnp.int32, count) // image_rows
    allowed = latent_image[None, None, :] <= images[:, None, None]
    new_max = jnp.maximum(running_max, jnp.max(jnp.where(allowed, scores, -1e30), axis=2))
    probs = jnp.exp(jnp.where(allowed, scores - new_max[:, :, None], -1e30))
    new_sum = jnp.sum(probs, axis=2)
    new_weighted = jnp.einsum(
        "thl,lhd->thd", probs.astype(jnp.bfloat16), value_heads, preferred_element_type=jnp.float32
    )
    return (new_max, new_sum, new_weighted)


def per_device(queries, keys, values, image_index, head_gate, out_weight):
    heads = head_gate.shape[0]
    tok_rows = queries.shape[1]
    query_heads = queries[0].reshape(tok_rows, heads, -1)
    head_size = query_heads.shape[2]
    images = image_index[0]
    image_rows = keys.shape[1] * lax.axis_size("blk") // IMAGES
    initial = (
        jnp.full((tok_rows, heads), -1e30, jnp.float32),
        jnp.zeros((tok_rows, heads), jnp.float32),
        jnp.zeros((tok_rows, heads, head_size), jnp.float32),
    )
    key_rows = lax.all_gather(keys, "blk", axis=1, tiled=True)[0]
    value_rows = lax.all_gather(values, "blk", axis=1, tiled=True)[0]
    state = update(initial, query_heads, images, key_rows, value_rows, image_rows)
    running_max, running_sum, weighted = state
    gate_value = jnp.tanh(head_gate)
    attended = weighted / running_sum[:, :, None] * gate_value[None, :, None]
    hidden = attended.reshape(tok_rows, -1).astype(jnp.bfloat16)
    projected = jnp.dot(
        hidden,
        lax.all_gather(out_weight, "blk", axis=1, tiled=True),
        preferred_element_type=jnp.float32,
    )
    return projected.astype(jnp.bfloat16)[None]


def solution(mesh):
    placed = (
        P("seq", "blk", None),
        P("seq", "blk", None),
        P("seq", "blk", None),
        P("seq", "blk"),
        P(),
        P(None, "blk"),
    )
    return jax.shard_map(
        per_device, mesh=mesh, in_specs=placed, out_specs=P("seq", "blk", None), check_vma=False
    )
```

profile of v0, /device:TPU:0, one launch (start us, length us, event | category | flops | bytes accessed | tf_op | source)
XLA Modules:
  0.0 227.8 jit_solution(4018921631297319439)
XLA Ops:
  6.5 0.0 copy-start.1
  6.5 0.0 copy-start
  6.5 0.0 all-gather.4.cloned.1.call-start
  6.5 0.7 all-gather.4.cloned.1.call-update
  7.3 0.0 all-gather.6.cloned.1.call-start
  7.3 0.7 all-gather.6.cloned.1.call-update
  8.0 0.0 all-gather.8.cloned.1.call-start
  8.1 0.7 all-gather.8.cloned.1.call-update
  8.7 1.4 copy.22
  10.2 0.0 copy-done.1
  10.2 0.0 copy-done
  10.2 0.1 broadcast_compare_fusion
  10.4 23.6 %all-gather.4.cloned.1.call-done = bf16[1,256,2048]{2,1,0:T(8,128)(2,1)} async-done(((bf16[1,32,2048]{2,1,0:T(8,128)(2,1)}), bf16[1,256,2048]{2,1,0:T(8,128)(2,1)}) %all-gather.4.cloned.1.call-update) | async-done | bytes 1048592 | tf_op jit(solution)/shard_map/all_gather | solution.py:42
  33.9 1.5 copy.15
  35.4 22.0 %all-gather.6.cloned.1.call-done = bf16[1,256,2048]{2,1,0:T(8,128)(2,1)} async-done(((bf16[1,32,2048]{2,1,0:T(8,128)(2,1)}), bf16[1,256,2048]{2,1,0:T(8,128)(2,1)}) %all-gather.6.cloned.1.call-update) | async-done | bytes 1048592 | tf_op jit(solution)/shard_map/all_gather | solution.py:43
  57.4 1.5 copy.18
  58.9 1.0 fusion.1
  59.9 0.9 fusion.4
  60.8 1.3 fusion.9
  62.1 147.6 %all-gather.8.cloned.1.call-done = bf16[2048,4096]{1,0:T(8,128)(2,1)} async-done(((bf16[2048,512]{1,0:T(8,128)(2,1)}), bf16[2048,4096]{1,0:T(8,128)(2,1)}) %all-gather.8.cloned.1.call-update) | async-done | bytes 16777232 | tf_op jit(solution)/shard_map/all_gather | solution.py:51
  209.7 11.5 %fusion = bf16[1,256,4096]{2,1,0:T(8,128)(2,1)} fusion(bf16[256,2048]{0,1:T(8,128)(2,1)S(1)} %bitcast.37, bf16[2048,4096]{1,0:T(8,128)(2,1)} %all-gather.8.cloned.1.call-done), kind=kOutput, calls=%fused_computation.1 | convolution fusion | flops 4296015872 | bytes 19922944 | tf_op jit(solution)/shard_map/dot_general | solution.py:49
  (3 shorter events, 0.0 us)
Async XLA Ops:
  6.5 3.7 %copy-start.1 = (f32[16]{0:T(128)S(1)}, f32[16]{0:T(128)}, u32[]{:S(2)}) copy-start(f32[16]{0:T(128)} %param.10) | copy-start | bytes 196
  6.5 3.7 %copy-start = (s32[1,256]{1,0:T(1,128)S(1)}, s32[1,256]{1,0:T(1,128)}, u32[]{:S(2)}) copy-start(s32[1,256]{1,0:T(1,128)} %param.9) | copy-start | bytes 3076
  6.5 27.4 %all-gather.4.cloned.1.call-start = ((), (), s32[]{:S(2)}) async-start(), calls=%async_computation | async-start | bytes 1179648 | tf_op jit(solution)/shard_map/all_gather | solution.py:42
  7.3 50.1 %all-gather.6.cloned.1.call-start = ((), (), s32[]{:S(2)}) async-start(), calls=%async_computation.1 | async-start | bytes 1179648 | tf_op jit(solution)/shard_map/all_gather | solution.py:43
  8.0 201.7 %all-gather.8.cloned.1.call-start = ((), (), s32[]{:S(2)}) async-start(), calls=%async_computation.2 | async-start | bytes 18874368 | tf_op jit(solution)/shard_map/all_gather | solution.py:51
Sparse Core Ops, SparseCore 0:
  8.9 24.9 all-gather.3
  35.5 21.8 all-gather.5
  59.0 150.6 all-gather.7
where the time goes:
time: 228 us
  waiting for transfers between devices  195 us (86%)
  matrix products  13.8 us (6%)
  between operations  13.2 us (6%)
  local copies, waits for them, and re-layouts  4.41 us (2%)
    all_gather x1, waiting for transfers between devices, per_device(): lax.all_gather(out_weight, 'blk', axis=1, tiled=True)  148 us
    all_gather x1, waiting for transfers between devices, per_device(): key_rows = lax.all_gather(keys, 'blk', axis=1, tiled=True)[0]  23.6 us
    all_gather x1, waiting for transfers between devices, per_device(): value_rows = lax.all_gather(values, 'blk', axis=1, tiled=True)[0]  22 us
    dot_general x1, matrix products, per_device(): jnp.dot(hidden, lax.all_gather(out_weight, 'blk', axis=1, tiled=True), pr...  11.5 us
  transfers between devices with their start and end apart: 3, of which 3 were waited for; matrix products, arithmetic and copies ran while one was open for 3% of the time, Pallas kernels for 0%

commit v1 on v0

--- a/solution.py
+++ b/solution.py
@@ -48,7 +48,7 @@
     hidden = attended.reshape(tok_rows, -1).astype(jnp.bfloat16)
     projected = jnp.dot(
         hidden,
-        lax.all_gather(out_weight, "blk", axis=1, tiled=True),
+        jnp.concatenate(lax.all_gather(out_weight, "blk"), axis=1),
         preferred_element_type=jnp.float32,
     )
     return projected.astype(jnp.bfloat16)[None]

time: 228 us -> 257 us (1.13)
  local copies, waits for them, and re-layouts: 4.41 us -> 26 us
  matrix products: 13.8 us -> 20.2 us
    reshape x0 -> x1, local copies, waits for them, and re-layouts: none -> 21.6 us  [per_device(): jnp.concatenate(lax.all_gather(out_weight, 'blk'), axis=1)]
    dot_general x1, matrix products: 11.5 us -> 17.9 us  [per_device(): jnp.dot(hidden, jnp.concatenate(lax.all_gather(out_weight, 'blk'), axis=1...]
where the time goes in v1:
time: 257 us; the launch traced here: 256 us
  waiting for transfers between devices  195 us (76%)
  local copies, waits for them, and re-layouts  26 us (10%)
  matrix products  20.2 us (8%)
  between operations  13.2 us (5%)
    all_gather x1, waiting for transfers between devices, per_device(): lax.all_gather(out_weight, 'blk')  148 us
    all_gather x1, waiting for transfers between devices, per_device(): key_rows = lax.all_gather(keys, 'blk', axis=1, tiled=True)[0]  23.6 us
    all_gather x1, waiting for transfers between devices, per_device(): value_rows = lax.all_gather(values, 'blk', axis=1, tiled=True)[0]  22 us
    reshape x1, local copies, waits for them, and re-layouts, per_device(): jnp.concatenate(lax.all_gather(out_weight, 'blk'), axis=1)  21.6 us
    dot_general x1, matrix products, per_device(): jnp.dot(hidden, jnp.concatenate(lax.all_gather(out_weight, 'blk'), axis=1...  17.9 us
  transfers between devices with their start and end apart: 3, of which 3 were waited for; matrix products, arithmetic and copies ran while one was open for 3% of the time, Pallas kernels for 0%

profile of v1, /device:TPU:0, one launch (start us, length us, event | category | flops | bytes accessed | tf_op | source)
XLA Modules:
  0.0 255.8 jit_solution(10253306595045270157)
XLA Ops:
  6.5 0.0 copy-start.1
  6.5 0.0 copy-start
  6.5 0.0 all-gather.5.cloned.1.call-start
  6.5 0.7 all-gather.5.cloned.1.call-update
  7.3 0.0 all-gather.7.cloned.1.call-start
  7.3 0.7 all-gather.7.cloned.1.call-update
  8.0 0.0 all-gather.9.cloned.1.call-start
  8.1 0.7 all-gather.9.cloned.1.call-update
  8.7 1.4 copy.29
  10.2 0.0 copy-done.1
  10.2 0.0 copy-done
  10.2 0.1 broadcast_compare_fusion
  10.4 23.6 %all-gather.5.cloned.1.call-done = bf16[1,256,2048]{2,1,0:T(8,128)(2,1)} async-done(((bf16[1,32,2048]{2,1,0:T(8,128)(2,1)}), bf16[1,256,2048]{2,1,0:T(8,128)(2,1)}) %all-gather.5.cloned.1.call-update) | async-done | bytes 1048592 | tf_op jit(solution)/shard_map/all_gather | solution.py:42
  33.9 1.5 copy.21
  35.4 22.0 %all-gather.7.cloned.1.call-done = bf16[1,256,2048]{2,1,0:T(8,128)(2,1)} async-done(((bf16[1,32,2048]{2,1,0:T(8,128)(2,1)}), bf16[1,256,2048]{2,1,0:T(8,128)(2,1)}) %all-gather.7.cloned.1.call-update) | async-done | bytes 1048592 | tf_op jit(solution)/shard_map/all_gather | solution.py:43
  57.4 1.5 copy.24
  58.9 1.0 fusion.1
  59.9 0.9 fusion.4
  60.8 1.3 fusion.9
  62.1 147.6 %all-gather.9.cloned.1.call-done = bf16[16384,512]{1,0:T(8,128)(2,1)} async-done(((bf16[2048,512]{1,0:T(8,128)(2,1)}), bf16[16384,512]{1,0:T(8,128)(2,1)}) %all-gather.9.cloned.1.call-update) | async-done | bytes 16777232 | tf_op jit(solution)/shard_map/all_gather | solution.py:51
  209.7 21.6 %copy.26 = bf16[2048,8,512]{0,2,1:T(8,128)(2,1)} copy(bf16[2048,8,512]{2,0,1:T(8,128)(2,1)} %bitcast.39) | data formatting | bytes 33554432 | tf_op jit(solution)/shard_map/reshape | solution.py:51
  231.3 17.9 %fusion = bf16[1,256,4096]{2,1,0:T(8,128)(2,1)} fusion(bf16[256,2048]{0,1:T(8,128)(2,1)S(1)} %bitcast.46, bf16[2048,4096]{0,1:T(8,128)(2,1)} %bitcast.40), kind=kOutput, calls=%fused_computation.1 | convolution fusion | flops 4296015872 | bytes 19922944 | tf_op jit(solution)/shard_map/dot_general | solution.py:49
  (3 shorter events, 0.0 us)
Async XLA Ops:
  6.5 3.7 %copy-start.1 = (f32[16]{0:T(128)S(1)}, f32[16]{0:T(128)}, u32[]{:S(2)}) copy-start(f32[16]{0:T(128)} %param.10) | copy-start | bytes 196
  6.5 3.7 %copy-start = (s32[1,256]{1,0:T(1,128)S(1)}, s32[1,256]{1,0:T(1,128)}, u32[]{:S(2)}) copy-start(s32[1,256]{1,0:T(1,128)} %param.9) | copy-start | bytes 3076
  6.5 27.4 %all-gather.5.cloned.1.call-start = ((), (), s32[]{:S(2)}) async-start(), calls=%async_computation | async-start | bytes 1179648 | tf_op jit(solution)/shard_map/all_gather | solution.py:42
  7.3 50.1 %all-gather.7.cloned.1.call-start = ((), (), s32[]{:S(2)}) async-start(), calls=%async_computation.1 | async-start | bytes 1179648 | tf_op jit(solution)/shard_map/all_gather | solution.py:43
  8.0 201.7 %all-gather.9.cloned.1.call-start = ((), (), s32[]{:S(2)}) async-start(), calls=%async_computation.2 | async-start | bytes 18874368 | tf_op jit(solution)/shard_map/all_gather | solution.py:51
Sparse Core Ops, SparseCore 0:
  8.9 24.9 all-gather.4
  35.5 21.8 all-gather.6
  59.0 150.6 all-gather.8
